TPU v7x, 256 devices: a 2x2x32 block of a 4x8x32 slice. The times are simulated.
256 devices in a mesh: band: 4 (over x, y), tm: 64 (over z, core).
Axes of the slice: x: 2, y: 2, z: 32, core: 2. Of those that a mesh axis runs over, the one named last changes fastest.
The devices are a block of a 4x8x32 slice.
Arguments:
- voltages: bfloat16 [32, 2, 512, 16384], P('band', None, None, 'tm'), parts along dimension 0, may hold values from -12 to 12
- antenna_flags: int32 [128, 32], P('tm', 'band'), parts along dimension 1, may hold values from -2147483648 to 2147483647, as said below
- owned_tile: int32 [64], replicated, may hold values from 0 to 63, each once
Outputs:
- visibility: float32 [512, 32, 2, 512], P('tm', 'band'), parts along dimension 1
There are 4 independent parts, one for each index of `band`. A program takes and returns all parts, laid end to end along the dimension named above; an argument that names none is the same for every part. Nothing has to cross between parts.
Inputs may be any that keep to these rules, and one draw needn't show every extreme that they name: `antenna_flags`: bit b of word w of sub-integration s is 1 where the samples of both polarisations of antenna 32 * w + b are good in that sub-integration of 128 samples, 0 where flagged; all 32 bits of a word are used; some antennas may be flagged in every sub-integration. A permutation: the index k of tm holds the baseline rows of tile owned_tile[k].
All inputs are finite; a program needn't handle non-finite values.
Results may differ from a plain program's by a relative error of at most 0.0003.
Values sent between devices are 32-bit elements; how exact they have to be, the bound alone decides.
A program may use at most 128 MiB of HBM per device.

v0:
```python
import jax
import jax.numpy as jnp
from jax import lax
from jax.sharding import Mesh
from jax.sharding import PartitionSpec as P

TM = ("tm_0", "tm_1")


def joined_along(pieces, dim):
    lengths = list(pieces.shape[1:])
    lengths[dim] *= pieces.shape[0]
    return jnp.moveaxis(pieces, 0, dim).reshape(lengths)


def stacked_from(array, axes, order):
    pieces = array[None]
    for k in order:
        pieces = lax.all_gather(pieces, axes[k], axis=0, tiled=True)
    block = [lax.axis_size(axes[k]) for k in reversed(order)]
    pieces = pieces.reshape(*block, *array.shape)
    turned = sorted(range(len(order)), key=lambda place: order[len(order) - 1 - place])
    return pieces.transpose(*turned, *range(len(order), pieces.ndim)).reshape(-1, *array.shape)


def gather_axes(array, axes, order, dim):
    return joined_along(stacked_from(array, axes, order), dim)


def own_block(pieces, axes, order):
    inside = pieces.shape[1:]
    pieces = pieces.reshape(*(lax.axis_size(a) for a in axes), *inside)
    pieces = jnp.moveaxis(pieces, order, range(len(axes))).reshape(-1, *inside)
    for k in order:
        pieces = lax.psum_scatter(pieces, axes[k], scatter_dimension=0, tiled=True)
    return pieces[0]


def in_blocks(array, dim, size):
    before, after = (array.shape[:dim], array.shape[dim + 1 :])
    return jnp.moveaxis(array.reshape(*before, size, -1, *after), dim, 0)


def summed_rows(array, axes, order, dim):
    size = lax.axis_size(axes)
    return own_block(in_blocks(array, dim, size), axes, order)


def unpack_flags(words):
    shifts = jnp.arange(32, dtype=jnp.int32)
    bits = jnp.bitwise_and(jnp.right_shift(words[:, :, None], shifts[None, None, :]), 1)
    return bits.reshape(words.shape[0], words.shape[1] * 32)


def stack_operands(masked):
    real_part = masked[:, 0]
    imag_part = masked[:, 1]
    right_side = jnp.concatenate([real_part, imag_part], axis=-1)
    left_side = jnp.stack([right_side, jnp.concatenate([imag_part, -real_part], axis=-1)], axis=1)
    return (left_side, right_side)


def shards(voltages, antenna_flags, owned_tile):
    axis_count = lax.axis_size(TM)
    my_index = lax.axis_index(TM)
    inputs = voltages.shape[2]
    samples = voltages.shape[3]
    block_rows = inputs // axis_count
    sub_length = samples // antenna_flags.shape[0]
    every_word = gather_axes(antenna_flags, TM, (0, 1), 0)
    every_flag = unpack_flags(every_word)
    local_flag = unpack_flags(antenna_flags)
    own_tile = owned_tile[my_index]
    own_antennas = (own_tile * block_rows + jnp.arange(block_rows, dtype=jnp.int32)) // 2
    own_flags = jnp.take(every_flag, own_antennas, axis=1)
    input_flags = jnp.repeat(every_flag, 2, axis=1)
    counts = sub_length * jnp.dot(own_flags.T, input_flags)
    divisor = jnp.maximum(counts, 1).astype(jnp.float32)[:, None, None, :]
    sample_flags = jnp.repeat(jnp.repeat(local_flag, 2, axis=1).T, sub_length, axis=1).astype(
        jnp.bfloat16
    )
    masked = voltages * sample_flags[None, None]
    left_side, right_side = stack_operands(masked)
    row_index = (
        owned_tile[:, None] * block_rows + jnp.arange(block_rows, dtype=jnp.int32)[None, :]
    ).reshape(-1)
    picked = jnp.take(left_side, row_index, axis=2)
    summed = summed_rows(
        jnp.einsum("ckru,cju->rckj", picked, right_side, preferred_element_type=jnp.float32),
        TM,
        (1, 0),
        0,
    )
    return summed / divisor


def solution(mesh):
    finer = Mesh(mesh.devices.reshape(mesh.shape["band"], 32, 2), ("band", "tm_0", "tm_1"))
    in_specs = (P("band", None, None, TM), P(TM, "band"), P())
    out_specs = P(TM, "band", None, None)
    return jax.shard_map(
        shards, mesh=finer, in_specs=in_specs, out_specs=out_specs, check_vma=False
    )
```

profile of v0, /device:TPU:46, one launch (start us, length us, event | category | flops | bytes accessed | tf_op | source)
XLA Modules:
  0.0 325.4 jit_solution(10085055809048941191)
XLA Ops:
  6.6 0.8 copy.16
  7.4 0.1 fusion.8
  7.6 0.6 broadcast_in_dim.40
  8.2 2.7 copy_multiply_fusion
  10.9 2.4 slice_bitcast_fusion.1
  13.3 0.1 fusion.15
  13.5 0.1 add.110
  13.7 5.3 %fusion.3 = (bf16[8,1,512,512]{3,2,0,1:T(8,128)(2,1)S(1)}, bf16[8,1,512,512]{3,2,0,1:T(8,128)(2,1)}) fusion(bf16[8,512,256]{2,1,0:T(8,128)(2,1)} %get-tuple-element.6, bf16[8,512,256]{2,1,0:T(8,128)(2,1)} %get-tuple-element.5, bf16[8,512,256]{2,1,0:T(8,128)(2,1)S(1)} %fusion.15), kind=kLoop, calls=%fused_computation.10 | loop fusion | flops 16777216 | bytes 14680064 | tf_op jit(solution)/shard_map/stack | solution.py:59
  19.0 6.2 %pad_maximum_fusion = bf16[8,2,512,512]{3,2,0,1:T(8,128)(2,1)} fusion(bf16[8,1,512,512]{3,2,0,1:T(8,128)(2,1)} %get-tuple-element.8, bf16[8,1,512,512]{3,2,0,1:T(8,128)(2,1)S(1)} %get-tuple-element.7), kind=kLoop, calls=%fused_computation.2 | loop fusion | flops 4194304 | bytes 16777216 | tf_op jit(solution)/shard_map/stack | solution.py:59
  25.1 11.3 %copy.18 = bf16[8,2,512,512]{3,0,2,1:T(8,128)(2,1)} copy(bf16[8,2,512,512]{3,2,0,1:T(8,128)(2,1)} %pad_maximum_fusion) | data formatting | bytes 16777216 | tf_op jit(solution)/shard_map/stack | solution.py:59
  36.5 23.2 %gather_fusion = bf16[512,8,2,512]{3,1,2,0:T(8,128)(2,1)} fusion(bf16[8,2,512,512]{3,0,2,1:T(8,128)(2,1)} %copy.18, s32[1024]{0:T(1024)S(1)} %pad_clamp_fusion.1), kind=kCustom, calls=%fused_computation | custom fusion | bytes 16779264 | tf_op jit(solution)/shard_map/jit(_take)/gather | solution.py:87
  59.8 7.8 %select_bitcast_fusion = bf16[8,2,512,512]{3,0,1,2:T(8,128)(2,1)} fusion(bf16[512,8,2,512]{3,1,2,0:T(8,128)(2,1)} %gather_fusion, pred[512]{0:T(512)(128)(4,1)S(1)} %compare_and_fusion.1), kind=kLoop, calls=%fused_computation.5 | loop fusion | flops 4194304 | bytes 16777728 | tf_op jit(solution)/shard_map/jit(_take)/select_n | solution.py:87
  67.5 19.3 %fusion = f32[8,512,2,512]{1,3,2,0:T(8,128)} fusion(bf16[8,2,512,512]{3,0,1,2:T(8,128)(2,1)} %select_bitcast_fusion, bf16[8,512,256]{2,1,0:T(8,128)(2,1)} %get-tuple-element.6, bf16[8,512,256]{2,1,0:T(8,128)(2,1)S(1)} %copy-done), kind=kOutput, calls=%fused_computation.3 | convolution fusion | flops 4303355904 | bytes 29360128 | tf_op jit(solution)/shard_map/ckru,cju->rckj/dot_general | solution.py:89
  86.8 20.4 %copy.20 = f32[2,32,8,8,2,512]{5,3,4,2,1,0:T(8,128)} copy(f32[2,32,8,8,2,512]{5,2,0,1,4,3:T(8,128)} %bitcast.54) | data formatting | bytes 33554432 | tf_op jit(solution)/shard_map/transpose | solution.py:33
  107.4 53.4 %reduce-scatter.3.cloned.1.call-done = f32[32,8,8,2,512]{4,2,3,1,0:T(8,128)} async-done(((f32[64,8,8,2,512]{4,2,3,1,0:T(8,128)}), f32[32,8,8,2,512]{4,2,3,1,0:T(8,128)}) %reduce-scatter.3.cloned.1.call-update) | async-done | bytes 8388624 | tf_op jit(solution)/shard_map/reduce_scatter | solution.py:35
  160.9 0.6 dynamic_slice.3
  161.5 56.5 %all-gather.1 = s32[32,2,8]{2,1,0:T(2,128)S(1)} all-gather(s32[1,2,8]{2,1,0:T(2,128)S(1)} %bitcast.62), channel_id=2, replica_groups=mesh['band'=4,'tm_0'=32,'tm_1'=2] {'tm_0'}, dimensions={0}, use_global_device_ids=true | all-gather | bytes 2112 | tf_op jit(solution)/shard_map/all_gather | solution.py:19
  218.0 1.9 all_gather.7
  219.9 0.1 fusion.6
  220.8 0.6 gather_fusion.1
  221.4 0.5 fusion.5
  221.9 94.8 %reduce-scatter.5.cloned.1.call-done = f32[1,8,8,2,512]{4,2,3,1,0:T(8,128)} async-done(((f32[32,8,8,2,512]{4,2,3,1,0:T(8,128)}), f32[1,8,8,2,512]{4,2,3,1,0:T(8,128)}) %reduce-scatter.5.cloned.1.call-update) | async-done | bytes 262160 | tf_op jit(solution)/shard_map/reduce_scatter | solution.py:35
  316.7 1.0 bitcast_divide_fusion
  317.7 0.9 copy.23
  (26 shorter events, 0.8 us)
Async XLA Ops:
  6.5 154.3 %reduce-scatter.3.cloned.1.call-start = ((), (), s32[]{:S(2)}) async-start(), calls=%async_computation.2 | async-start | bytes 25165824 | tf_op jit(solution)/shard_map/reduce_scatter | solution.py:35
  10.9 2.5 copy-start.2
  59.7 7.8 %copy-start = (bf16[8,512,256]{2,1,0:T(8,128)(2,1)S(1)}, bf16[8,512,256]{2,1,0:T(8,128)(2,1)}, u32[]{:S(2)}) copy-start(bf16[8,512,256]{2,1,0:T(8,128)(2,1)} %get-tuple-element.5) | copy-start | bytes 6291460
  107.3 209.4 %reduce-scatter.5.cloned.1.call-start = ((), (), s32[]{:S(2)}) async-start(), calls=%async_computation.3 | async-start | bytes 8650752 | tf_op jit(solution)/shard_map/reduce_scatter | solution.py:35
  160.8 0.7 copy-start.1
Sparse Core Ops, SparseCore 0:
  107.4 53.3 reduce-scatter.2
  163.4 153.2 reduce-scatter.4
where the time goes:
time: 326 us; the launch traced here: 325 us
  waiting for transfers between devices  148 us (45%)
  local copies, waits for them, and re-layouts  61.3 us (19%)
  blocking collectives  58.4 us (18%)
  other arithmetic  23.4 us (7%)
  matrix products  19.8 us (6%)
  between operations  14.2 us (4%)
    reduce_scatter x2, waiting for transfers between devices, own_block(): pieces = lax.psum_scatter(pieces, axes[k], scatter_dimension=0, tiled=True)  148 us
    all_gather x2, blocking collectives, stacked_from(): pieces = lax.all_gather(pieces, axes[k], axis=0, tiled=True)  58.4 us
    gather x1, local copies, waits for them, and re-layouts, shards(): picked = jnp.take(left_side, row_index, axis=2)  23.2 us
    transpose x1, local copies, waits for them, and re-layouts, own_block(): pieces = jnp.moveaxis(pieces, order, range(len(axes))).reshape(-1, *inside)  20.4 us
    dot_general x1, matrix products, shards(): jnp.einsum('ckru,cju->rckj', picked, right_side, preferred_element_type=j...  19.3 us
    another operation x2, other arithmetic, stack_operands(): jnp.stack([right_side, jnp.concatenate([imag_part, -real_part], axis=-1)]...  11.5 us
    another operation x1, local copies, waits for them, and re-layouts, stack_operands(): jnp.stack([right_side, jnp.concatenate([imag_part, -real_part], axis=-1)]...  11.3 us
    select_n x2, other arithmetic, shards(): picked = jnp.take(left_side, row_index, axis=2)  7.78 us
  transfers between devices with their start and end apart: 2, of which 2 were waited for; matrix products, arithmetic and copies ran while one was open for 1% of the time, Pallas kernels for 0%

commit v1 on v0

v1 whole, which is shorter than its diff:
```python
import functools

import jax
import jax.numpy as jnp
from jax import lax
from jax.experimental import pallas as pl
from jax.experimental.pallas import tpu as pltpu
from jax.sharding import PartitionSpec as P

MESH = pl.DeviceIdType.MESH
F32 = jnp.float32
BF16 = jnp.bfloat16
LANES = 128
WORD = 32


def dot_nt(a, b):
    return lax.dot_general(a, b, (((1,), (1,)), ((), ())), preferred_element_type=F32)


def bit_of(words, shifts):
    return jnp.bitwise_and(lax.shift_right_logical(words, shifts), 1)


def iota(shape, dim):
    return lax.broadcasted_iota(jnp.int32, shape, dim)


def swap_chunks(blocks, width):
    count = len(blocks)
    lanes = count * width
    blocks = list(blocks)
    stride = count // 2
    while stride:
        chunk = lax.div(iota(blocks[0].shape, 1), width)
        low = jnp.bitwise_and(chunk, stride) == 0
        for i in range(count):
            if i & stride:
                continue
            a, b = blocks[i], blocks[i + stride]
            blocks[i] = jnp.where(low, a, pltpu.roll(b, stride * width, 1))
            blocks[i + stride] = jnp.where(low, pltpu.roll(a, lanes - stride * width, 1), b)
        stride //= 2
    return blocks


def kernel(
    n, tiles, flags, v_hbm, out, *refs
):
    channels = v_hbm.shape[0]
    vbuf = refs[:channels]
    (
        mask, x, onehot, ring_m, ring_e, sib_m, sib_e, own_m, own_e, snd_m, snd_e, turned, exch, final, arrived,
        vsem, ring_send, ring_recv, sib_send, sib_recv, exch_send, exch_recv, fin_send, fin_recv,
    ) = refs[channels:]
    parts, _, block, samples = vbuf[0].shape
    half_ch = channels // 2
    subs = flags.shape[0]
    sub_len = samples // subs
    rows = 2 * block
    inputs = n * rows
    hops = n // 2
    window = hops * rows
    ants = block // 2
    per_word = WORD // ants
    group = parts * rows

    me = lax.axis_index("tm")
    z = lax.div(me, 2)
    core = lax.rem(me, 2)
    sigma = 1 - 2 * core
    other = 1 - core

    def wrap(k):
        return lax.rem(k + 2 * n, n)

    def device(chip, which):
        return {"tm": 2 * chip + which}

    ahead = (device(wrap(z + sigma), core), device(wrap(z - sigma), core))
    sibling = device(z, other)

    def v_copy(c):
        return pltpu.make_async_copy(v_hbm.at[c], vbuf[c], vsem.at[c])

    for c in range(channels):
        v_copy(c).start()

    barrier = pltpu.get_barrier_semaphore()
    for peer in (*ahead, sibling):
        pl.semaphore_signal(barrier, inc=1, device_id=peer, device_id_type=MESH)

    row = iota((rows, LANES), 0)
    upper = row >= block

    def make_mask(q, _):
        t0, t1 = tiles[2 * q], tiles[2 * q + 1]
        shift = jnp.where(upper, lax.rem(t1, per_word) * ants, lax.rem(t0, per_word) * ants) + lax.div(lax.rem(row, block), 2)
        for s in range(subs):
            words = jnp.where(upper, flags[s, lax.div(t1, per_word)], flags[s, lax.div(t0, per_word)])
            mask[s, pl.ds(pl.multiple_of(q * rows, rows), rows), :] = bit_of(words, shift).astype(F32).astype(BF16)
        return 0

    lax.fori_loop(0, n, make_mask, 0)

    cs, cl = iota((2 * ants, LANES), 0), iota((2 * ants, LANES), 1)
    column_bits = []
    for s in range(subs):
        words = jnp.zeros((2 * ants, LANES), jnp.int32)
        for w in range(flags.shape[1]):
            here = (lax.div(cs, ants) * (LANES // WORD) + lax.div(cl, WORD)) == w
            words = jnp.where(here, flags[s, w], words)
        column_bits.append(bit_of(words, lax.rem(cl, WORD)))

    def place(c, q, again):
        t0, t1 = tiles[2 * q], tiles[2 * q + 1]
        at = pl.multiple_of(q * rows, rows)
        for p in range(parts):
            value = jnp.concatenate([vbuf[c][p, t0], vbuf[c][p, t1]], axis=0)
            for s in range(subs):
                piece = value[:, s * sub_len : (s + 1) * sub_len] * mask[s, pl.ds(at, rows), :]
                lanes = pl.ds(p * samples + s * sub_len, sub_len)
                x[c, pl.ds(at, rows), lanes] = piece
                if again:
                    x[c, pl.ds(pl.multiple_of(inputs + at, rows), rows), lanes] = piece

    for c in range(channels):
        v_copy(c).wait()
        lax.fori_loop(0, hops, lambda q, _: (place(c, q, True), 0)[1], 0, unroll=2)
        lax.fori_loop(hops, n, lambda q, _: (place(c, q, False), 0)[1], 0, unroll=2)

    def quarter(held):
        return jnp.concatenate([held, jnp.concatenate([held[:, samples:], -held[:, :samples]], axis=1)], axis=0)

    def destination(which, direction, s):
        step = (hops - s) * (1 - 2 * which) * (1 - 2 * direction)
        return wrap(z + step)

    def window_chip(which, chip):
        return wrap(chip - which * (hops - 1))

    def add_channel(which, direction, s, c, main):
        chip = destination(which, direction, s)
        ch = which * half_ch + c
        held = x[ch, pl.ds(pl.multiple_of(chip * rows, rows), rows), :]
        start = window_chip(which, chip) * rows
        wide = x[ch, pl.ds(pl.multiple_of(start, rows), window), :]
        main[direction, s, c * group : (c + 1) * group, :] = dot_nt(quarter(held), wide)

    def add_extra(which, direction, s, extra):
        chip = destination(which, direction, s)
        total = jnp.zeros((rows, half_ch * group), F32)
        for c in range(half_ch):
            ch = which * half_ch + c
            held = x[ch, pl.ds(pl.multiple_of(chip * rows, rows), rows), :]
            far = quarter(x[ch, pl.ds(pl.multiple_of(wrap(chip + hops) * rows, rows), rows), :])
            pieces = [far]
            if c:
                pieces.insert(0, jnp.zeros((c * group, far.shape[1]), BF16))
            if c < half_ch - 1:
                pieces.append(jnp.zeros(((half_ch - 1 - c) * group, far.shape[1]), BF16))
            total += dot_nt(held, jnp.concatenate(pieces, axis=0))
        extra[direction, s, 0:rows, :] = total
        t = tiles[2 * chip + which]
        shift = lax.rem(t, per_word) * ants + lax.rem(cs, ants)
        pairs = jnp.zeros((2 * ants, LANES), jnp.int32)
        for k in range(subs):
            words = jnp.zeros((2 * ants, LANES), jnp.int32) + flags[k, lax.div(t, per_word)]
            pairs += bit_of(words, shift) * column_bits[k]
        extra[direction, s, rows : rows + 2 * ants, :] = (pairs * sub_len).astype(F32)

    def sib_copies(direction, s):
        return [
            pltpu.make_async_remote_copy(
                src_ref=src.at[direction, s], dst_ref=dst.at[direction, s],
                send_sem=sib_send.at[direction, s, k], recv_sem=sib_recv.at[direction, s, k],
                device_id=sibling, device_id_type=MESH,
            )
            for k, (src, dst) in enumerate(((snd_m, sib_m), (snd_e, sib_e)))
        ]

    def send_sibling(direction, s):
        for copy in sib_copies(direction, s):
            copy.start()

    def whole(which, direction, s, main, extra):
        for c in range(half_ch):
            add_channel(which, direction, s, c, main)
        add_extra(which, direction, s, extra)

    def slot(direction, s, k):
        if k < half_ch:
            return [r.at[direction, s, pl.ds(k * group, group), :] for r in (ring_m, own_m, sib_m)]
        return [r.at[direction, s] for r in (ring_e, own_e, sib_e)]

    def ring_copy(direction, s, k):
        return pltpu.make_async_remote_copy(
            src_ref=slot(direction, s, k)[0], dst_ref=slot(direction, s + 1, k)[0],
            send_sem=ring_send.at[direction, k], recv_sem=ring_recv.at[direction, s + 1, k],
            device_id=ahead[direction], device_id_type=MESH,
        )

    def relay(direction, s, k, first):
        if not first:
            ring_copy(direction, s - 1, k).wait_recv()
        if k == 0 or k == half_ch:
            sib_copies(direction, s)[min(k, 1)].wait_recv()
        held, mine, theirs = slot(direction, s, k)
        if first:
            held[...] = mine[...] + theirs[...]
        else:
            held[...] = held[...] + (mine[...] + theirs[...])
            ring_copy(direction, s - 1, k).wait_send()
        ring_copy(direction, s, k).start()

    pl.semaphore_wait(barrier, 3)

    whole(other, 0, 0, snd_m, snd_e)
    send_sibling(0, 0)
    whole(core, 0, 0, own_m, own_e)

    def early(direction, _):
        whole(other, direction, 1, snd_m, snd_e)
        send_sibling(direction, 1)
        whole(core, direction, 1, own_m, own_e)
        return 0

    for k in range(half_ch + 1):
        relay(0, 0, k, True)
    lax.fori_loop(0, 2, early, 0)

    def one_hot(q, _):
        first = window_chip(core, z)
        chip = jnp.where(q < hops, wrap(first + q), wrap(z - sigma * (q - hops + 1)))
        t0, t1 = tiles[2 * chip], tiles[2 * chip + 1]
        wide_row, wide_lane = iota((rows, inputs), 0), iota((rows, inputs), 1)
        goal = jnp.where(wide_row < block, t0, t1) * block + lax.rem(wide_row, block)
        onehot[pl.ds(pl.multiple_of(q * rows, rows), rows), :] = jnp.where(wide_lane == goal, 1.0, 0.0).astype(BF16)
        return 0

    def step(s, first, last):
        directions = (0,) if first == 0 else (0, 1)
        ahead_of = s + 2
        for k in range(half_ch):
            for d in directions:
                relay(d, s, k, d == first)
            for d in range(last):
                add_channel(other, d, ahead_of, k, snd_m)
                add_channel(core, d, ahead_of, k, own_m)
        for d in directions:
            relay(d, s, half_ch, d == first)
        for d in range(last):
            add_extra(other, d, ahead_of, snd_e)
            send_sibling(d, ahead_of)
            add_extra(core, d, ahead_of, own_e)

    def ahead_only(direction, _):
        whole(other, direction, 2, snd_m, snd_e)
        send_sibling(direction, 2)
        whole(core, direction, 2, own_m, own_e)
        return 0

    lax.fori_loop(0, 2, ahead_only, 0)
    step(1, 1, 2)
    lax.fori_loop(0, n, one_hot, 0)
    lax.fori_loop(2, hops - 2, lambda s, _: (step(s, None, 2), 0)[1], 0)
    step(hops - 2, None, 1)
    step(hops - 1, None, 0)

    for copy in sib_copies(0, hops):
        copy.wait_recv()
    for d in range(2):
        for k in range(half_ch + 1):
            ring_copy(d, hops - 1, k).wait_recv()
    near = ring_m[0, hops] + ring_m[1, hops] + (own_m[0, hops] + sib_m[0, hops])
    extra = ring_e[0, hops] + ring_e[1, hops] + (own_e[0, hops] + sib_e[0, hops])
    turned[...] = near.T.reshape(hops, rows, half_ch * group)

    def exchange(d):
        slab = jnp.where(core == 0, d, hops - 1 - d)
        return pltpu.make_async_remote_copy(
            src_ref=turned.at[slab], dst_ref=exch.at[d - 1],
            send_sem=exch_send.at[d - 1], recv_sem=exch_recv.at[d - 1],
            device_id=device(wrap(z + sigma * d), core), device_id_type=MESH,
        )

    for d in range(hops - 1, 0, -1):
        exchange(d).start()

    def replaced(value, at):
        total = None
        for _ in range(3):
            part = value.astype(BF16)
            value = value - part.astype(F32)
            moved = jnp.dot(part, onehot[at : at + window, :], preferred_element_type=F32)
            total = moved if total is None else total + moved
        return total

    result = replaced(near, 0)
    for d in range(1, hops):
        exchange(d).wait_recv()
    blocks = [exch[d] for d in range(hops - 1)] + [extra[0:rows]]
    pairs = half_ch * parts
    mirrored = []
    for g in range(hops // pairs):
        mirrored.append(swap_chunks(blocks[g * pairs : (g + 1) * pairs], rows))
    far = []
    for k in range(pairs):
        line = jnp.concatenate([m[k] for m in mirrored], axis=1)
        far.append(-line if k % parts else line)
    result = result + replaced(jnp.concatenate(far, axis=0), window)
    for k in range(pairs):
        for t in range(2):
            final[t, k] = result[k * rows + t * block : k * rows + (t + 1) * block]

    finish = pltpu.make_async_remote_copy(
        src_ref=final.at[other], dst_ref=arrived, send_sem=fin_send, recv_sem=fin_recv,
        device_id=sibling, device_id_type=MESH,
    )
    finish.start()

    counts = extra[rows : rows + 2 * ants]
    out_row = iota((block, LANES), 0)
    spread_row, spread_col = iota((LANES, 2 * LANES), 0), iota((LANES, 2 * LANES), 1)
    spread = jnp.where(lax.div(spread_col, 2) == spread_row, 1.0, 0.0).astype(BF16)
    wide = []
    for h in range(2):
        picked = jnp.zeros((block, LANES), F32)
        for a in range(ants):
            line = counts[h * ants + a : h * ants + a + 1, :]
            picked = jnp.where(lax.div(out_row, 2) == a, jnp.broadcast_to(line, picked.shape), picked)
        wide.append(jnp.dot(picked.astype(BF16), spread, preferred_element_type=F32))
    divisor = jnp.maximum(jnp.concatenate(wide, axis=1)[:, :inputs], 1.0)

    for k in range(pairs):
        out[core * pairs + k] = final[core, k] / divisor
    finish.wait()
    for k in range(pairs):
        out[other * pairs + k] = arrived[k] / divisor

    for d in range(1, hops):
        exchange(d).wait_send()
    for d in range(2):
        for k in range(half_ch + 1):
            ring_copy(d, hops - 1, k).wait_send()

    def sent(s, _):
        for d in range(2):
            for copy in sib_copies(d, s):
                copy.wait_send()
        return 0

    for copy in sib_copies(0, 0) + sib_copies(0, hops):
        copy.wait_send()
    lax.fori_loop(1, hops, sent, 0)


def shards(n, voltages, antenna_flags, owned_tile):
    channels, parts, inputs, samples = voltages.shape
    tiles = owned_tile.shape[0]
    block = inputs // tiles
    rows = 2 * block
    hops = n // 2
    window = hops * rows
    half = channels // 2
    lanes = half * parts * rows
    extra = rows + block
    subs = antenna_flags.shape[0]
    slots = hops + 1
    dma = pltpu.SemaphoreType.DMA
    main_slots = pltpu.VMEM((2, slots, lanes, window), F32)
    extra_slots = pltpu.VMEM((2, slots, extra, lanes), F32)
    smem = pl.BlockSpec(memory_space=pltpu.SMEM)
    summed = pl.pallas_call(
        functools.partial(kernel, n),
        out_shape=jax.ShapeDtypeStruct((channels * parts, block, inputs), F32),
        in_specs=[smem, smem, pl.BlockSpec(memory_space=pl.ANY)],
        out_specs=pl.BlockSpec(memory_space=pltpu.VMEM),
        scratch_shapes=[
            *[pltpu.VMEM((parts, tiles, block, samples), BF16)] * channels,
            pltpu.VMEM((subs, inputs, LANES), BF16),
            pltpu.VMEM((channels, inputs + window, parts * samples), BF16),
            pltpu.VMEM((inputs, inputs), BF16),
            main_slots, extra_slots,
            main_slots, extra_slots,
            main_slots, extra_slots,
            main_slots, extra_slots,
            pltpu.VMEM((hops, rows, lanes), F32),
            pltpu.VMEM((hops - 1, rows, lanes), F32),
            pltpu.VMEM((2, half * parts, block, inputs), F32),
            pltpu.VMEM((half * parts, block, inputs), F32),
            dma((channels,)),
            dma((2, half + 1)),
            dma((2, slots, half + 1)),
            dma((2, slots, 2)),
            dma((2, slots, 2)),
            dma((hops - 1,)),
            dma((hops - 1,)),
            dma,
            dma,
        ],
        compiler_params=pltpu.CompilerParams(
            collective_id=0, has_side_effects=True, vmem_limit_bytes=60 * 1024 * 1024
        ),
    )(owned_tile, antenna_flags, voltages.reshape(channels, parts, tiles, block, samples))
    return summed.reshape(channels, parts, block, inputs).transpose(2, 0, 1, 3)


def solution(mesh):
    in_specs = (P("band", None, None, "tm"), P("tm", "band"), P())
    out_specs = P("tm", "band", None, None)
    return jax.shard_map(
        functools.partial(shards, mesh.shape["tm"] // 2),
        mesh=mesh, in_specs=in_specs, out_specs=out_specs, check_vma=False,
    )
```

time: 326 us -> 117 us (0.36)
  the two profiles are of different devices: /device:TPU:46 before, /device:TPU:37 now
where the time goes in v1:
time: 117 us
  Pallas kernels  115 us (98%)
  local copies, waits for them, and re-layouts  1.86 us (2%)
    pallas_call x1, Pallas kernels, shards(): pl.pallas_call(functools.partial(kernel, n), out_shape=jax.ShapeDtypeStru...  115 us

profile of v1, /device:TPU:37, one launch (start us, length us, event | category | flops | bytes accessed | tf_op | source)
XLA Modules:
  0.0 117.0 jit_solution(5078335296895769953)
XLA Ops:
  0.0 115.2 %shard_map.37 = f32[16,8,512]{2,1,0:T(8,128)} custom-call(s32[64]{0:T(128)} %tiles.1, s32[2,8]{1,0:T(2,128)} %flags.1, bf16[8,2,64,8,256]{4,3,2,1,0:T(8,128)(2,1)} %bitcast.5), custom_call_target="tpu_custom_call" | custom-call | tf_op jit(solution)/shard_map/pallas_call | solution.py:374
  115.2 1.9 %copy.6 = f32[8,2,8,512]{3,1,0,2:T(2,128)} copy(f32[8,2,8,512]{3,2,1,0:T(8,128)} %bitcast.6) | data formatting | bytes 524288 | tf_op jit(solution)/shard_map/reshape | solution.py:406
